TPU v7x, 32 devices: a whole 2x2x4 slice. The times are simulated.
32 devices in a mesh: krow: 16 (over z, x, core), kcol: 2 (over y).
Axes of the slice: x: 2, y: 2, z: 4, core: 2. Of those that a mesh axis runs over, the one named last changes fastest.
Arguments:
- green: bfloat16 [4, 2, 16, 4, 256, 256], P(None, None, 'krow', 'kcol'), may hold values from -6 to 6
- screened: float32 [16, 4, 65536], P(None, None, ('krow', 'kcol')), may hold values from 0.1 to 1
Outputs:
- sigma: bfloat16 [4, 2, 16, 4, 256, 256], P(None, None, 'krow', 'kcol')
- dressed: bfloat16 [4, 2, 16, 4, 256, 256], P(None, None, 'krow', 'kcol')
All inputs are finite; a program needn't handle non-finite values.
Results may differ from a plain program's by a relative error of at most 0.0053.
Values may be sent and summed in bfloat16 or wider, within the bound.
A program may use at most 64 MiB of HBM per device.

v0:
```python
import functools
import math

import jax
import jax.numpy as jnp
from jax import lax
from jax.experimental import pallas as pl
from jax.experimental.pallas import tpu as pltpu
from jax.sharding import PartitionSpec as P

SUBLANES = 8
LANES = 128


def turn(values, count, size, sign):
    real, imag = values
    count = count * sign % size
    if count * 8 % size == 0:
        eighth = count * 8 // size
        half = math.sqrt(0.5)
        if eighth == 0:
            return real, imag
        if eighth == 2:
            return -imag, real
        if eighth == 4:
            return -real, -imag
        if eighth == 6:
            return imag, -real
        if eighth == 1:
            return (real - imag) * half, (real + imag) * half
        if eighth == 3:
            return (real + imag) * -half, (real - imag) * half
        if eighth == 5:
            return (imag - real) * half, (real + imag) * -half
        return (real + imag) * half, (imag - real) * half
    angle = 2.0 * math.pi * count / size
    cosine, sine = math.cos(angle), math.sin(angle)
    return real * cosine - imag * sine, real * sine + imag * cosine


def transform(values, sign):
    size = len(values)
    if size == 1:
        return values
    if size % 2:
        out = []
        for target in range(size):
            terms = [turn(v, target * source, size, sign) for source, v in enumerate(values)]
            out.append((sum(t[0] for t in terms), sum(t[1] for t in terms)))
        return out
    even = transform(values[0::2], sign)
    odd = transform(values[1::2], sign)
    low, high = [], []
    for t in range(size // 2):
        real, imag = turn(odd[t], t, size, sign)
        low.append((even[t][0] + real, even[t][1] + imag))
        high.append((even[t][0] - real, even[t][1] - imag))
    return low + high


def kernel(
    grid_dims, mesh_dims, rows,
    green, weights, sigma, dressed,
    arrived, results, middle,
    out_sems, in_sems, back_out_sems, back_in_sems,
):
    one, two = grid_dims
    row_count, column_count = mesh_dims
    devices = row_count * column_count
    energies, _, local, orbitals, _ = green.shape
    local_one, local_two = one // row_count, two // column_count
    my_row, my_column = lax.axis_index("krow"), lax.axis_index("kcol")
    me = my_row * column_count + my_column

    def place(peer):
        return (lax.div(peer, column_count), lax.rem(peer, column_count))

    def strip(owner):
        return pl.ds(pl.multiple_of(owner * rows, rows), rows)

    barrier = pltpu.get_barrier_semaphore()

    @pl.loop(1, devices)
    def _(step):
        pl.semaphore_signal(
            barrier, inc=1, device_id=place(lax.rem(me + step, devices)),
            device_id_type=pl.DeviceIdType.MESH,
        )

    pl.semaphore_wait(barrier, devices - 1)

    @pl.loop(0, energies)
    def _(e):
        @pl.loop(1, devices)
        def _(step):
            peer = lax.rem(me + step, devices)
            pltpu.make_async_remote_copy(
                src_ref=green.at[e, :, :, strip(peer), :],
                dst_ref=arrived.at[e, me],
                send_sem=out_sems.at[e],
                recv_sem=in_sems.at[e],
                device_id=place(peer),
                device_id_type=pl.DeviceIdType.MESH,
            ).start()

    def wait_all(buffer, sem, e):
        part = buffer.at[e, pl.ds(0, devices - 1)]
        pltpu.make_async_copy(part, part, sem.at[e]).wait()

    def slot(k1, k2):
        return (
            (k1 // local_one) * column_count + k2 // local_two,
            (k1 % local_one) * local_two + k2 % local_two,
        )

    scale = -1.0 / (one * two)

    @pl.loop(0, energies)
    def _(e):
        wait_all(arrived, in_sems, e)
        arrived[e, me] = green[e, :, :, strip(me), :]

        @pl.loop(0, orbitals // LANES)
        def _(h):
            lanes = pl.ds(pl.multiple_of(h * LANES, LANES), LANES)
            for k2 in range(two):
                values = []
                for k1 in range(one):
                    s, at = slot(k1, k2)
                    values.append(tuple(
                        arrived[e, s, c, at, :, lanes].astype(jnp.float32) for c in range(2)
                    ))
                for r1, v in enumerate(transform(values, 1)):
                    middle[r1, k2, 0] = v[0]
                    middle[r1, k2, 1] = v[1]
            for r1 in range(one):
                values = transform([(middle[r1, k2, 0], middle[r1, k2, 1]) for k2 in range(two)], 1)
                for r2 in range(two):
                    weight = weights[r1, r2, :, lanes] * scale
                    values[r2] = (values[r2][0] * weight, values[r2][1] * weight)
                for k2, v in enumerate(transform(values, -1)):
                    middle[r1, k2, 0] = v[0]
                    middle[r1, k2, 1] = v[1]
            for k2 in range(two):
                values = [(middle[r1, k2, 0], middle[r1, k2, 1]) for r1 in range(one)]
                for k1, v in enumerate(transform(values, -1)):
                    s, at = slot(k1, k2)
                    for c in range(2):
                        results[e, s, c, at, :, lanes] = v[c].astype(jnp.bfloat16)

        @pl.loop(1, devices)
        def _(step):
            peer = lax.rem(me + step, devices)
            pltpu.make_async_remote_copy(
                src_ref=results.at[e, peer],
                dst_ref=sigma.at[e, :, :, strip(me), :],
                send_sem=back_out_sems.at[e],
                recv_sem=back_in_sems.at[e],
                device_id=place(peer),
                device_id_type=pl.DeviceIdType.MESH,
            ).start()

        sigma[e, :, :, strip(me), :] = results[e, me]

    def times(left, right):
        return jnp.dot(left, right, preferred_element_type=jnp.float32)

    @pl.loop(0, energies)
    def _(e):
        wait_all(results, back_in_sems, e)

        @pl.loop(0, local)
        def _(at):
            g_real, g_imag = green[e, 0, at], green[e, 1, at]
            s_real, s_imag = sigma[e, 0, at], sigma[e, 1, at]
            kern_real = (times(g_real, s_real) - times(g_imag, s_imag)).astype(jnp.bfloat16)
            kern_imag = (times(g_real, s_imag) + times(g_imag, s_real)).astype(jnp.bfloat16)
            corr_real = times(kern_real, g_real) - times(kern_imag, g_imag)
            corr_imag = times(kern_real, g_imag) + times(kern_imag, g_real)
            share = 1.0 / orbitals
            dressed[e, 0, at] = (g_real.astype(jnp.float32) + corr_real * share).astype(jnp.bfloat16)
            dressed[e, 1, at] = (g_imag.astype(jnp.float32) + corr_imag * share).astype(jnp.bfloat16)

    @pl.loop(0, energies)
    def _(e):
        wait_all(arrived, out_sems, e)
        wait_all(results, back_out_sems, e)


def exchange_in_kernel(green, screened):
    mesh_dims = (lax.axis_size("krow"), lax.axis_size("kcol"))
    devices = mesh_dims[0] * mesh_dims[1]
    energies, _, local_one, local_two, orbitals, _ = green.shape
    grid_dims = screened.shape[:2]
    rows = orbitals // devices
    local = local_one * local_two
    flat = (energies, 2, local, orbitals, orbitals)
    weights = screened.reshape(grid_dims + (rows, orbitals))
    block = (energies, devices, 2, local, rows, orbitals)
    vmem = pl.BlockSpec(memory_space=pltpu.VMEM)
    sigma, dressed = pl.pallas_call(
        functools.partial(kernel, grid_dims, mesh_dims, rows),
        out_shape=[jax.ShapeDtypeStruct(flat, jnp.bfloat16)] * 2,
        in_specs=[vmem, vmem],
        out_specs=[vmem, vmem],
        scratch_shapes=[
            pltpu.VMEM(block, jnp.bfloat16),
            pltpu.VMEM(block, jnp.bfloat16),
            pltpu.VMEM(grid_dims + (2, rows, LANES), jnp.float32),
            pltpu.SemaphoreType.DMA((energies,)),
            pltpu.SemaphoreType.DMA((energies,)),
            pltpu.SemaphoreType.DMA((energies,)),
            pltpu.SemaphoreType.DMA((energies,)),
        ],
        compiler_params=pltpu.CompilerParams(collective_id=0, has_side_effects=True),
    )(green.reshape(flat), weights)
    return sigma.reshape(green.shape), dressed.reshape(green.shape)


full_turn = 2.0 * math.pi


def phase_tables(length, forward):
    step_counter = jnp.arange(length, dtype=jnp.int32)
    product = step_counter[:, None] * step_counter[None, :] % length
    angles = full_turn * product.astype(jnp.float32) / length
    if forward:
        return (jnp.cos(angles) / length, jnp.sin(angles) / length)
    return (jnp.cos(angles), -jnp.sin(angles))


def apply_over_axis(matrix, values, along_dim):
    letters = "abcdefgh"[: values.ndim]
    target = letters[:along_dim] + "z" + letters[along_dim + 1 :]
    formula = "z" + letters[along_dim] + "," + letters + "->" + target
    return jnp.einsum(formula, matrix, values, precision=lax.Precision.HIGHEST)


def complex_along(state, cosine, sine, along_dim):
    real_part, imag_part = state
    out_real = apply_over_axis(cosine, real_part, along_dim) - apply_over_axis(
        sine, imag_part, along_dim
    )
    out_imag = apply_over_axis(sine, real_part, along_dim) + apply_over_axis(
        cosine, imag_part, along_dim
    )
    return (out_real, out_imag)


def weigh_back(state, weights, lead_one, lead_two):
    state = (-weights * state[0], -weights * state[1])
    cos_one, sin_one = phase_tables(lead_one, False)
    state = complex_along(state, cos_one, sin_one, 1)
    cos_two, sin_two = phase_tables(lead_two, False)
    state = complex_along(state, cos_two, sin_two, 2)
    return jnp.stack(state, 1).astype(jnp.bfloat16)


def whole_local(pieces, weights):
    state = (pieces[:, 0].astype(jnp.float32), pieces[:, 1].astype(jnp.float32))
    cos_two, sin_two = phase_tables(pieces.shape[3], True)
    state = complex_along(state, cos_two, sin_two, 2)
    cos_one, sin_one = phase_tables(pieces.shape[2], True)
    state = complex_along(state, cos_one, sin_one, 1)
    return weigh_back(state, weights, pieces.shape[2], pieces.shape[3])


def matmul_batch(left, right):
    return jnp.einsum("eklij,ekljm->eklim", left, right, preferred_element_type=jnp.float32)


def per_device(green, screened):
    krow_count = lax.axis_size("krow")
    momentum_column_count = lax.axis_size("kcol")
    orbitals = green.shape[4]
    slice_len = orbitals * green.shape[5] // (krow_count * momentum_column_count)
    blocks = green.reshape(green.shape[:4] + (krow_count, momentum_column_count, slice_len))
    weights = screened.reshape(screened.shape[0], screened.shape[1], 1, 1, screened.shape[2])
    gathered = lax.all_to_all(
        lax.all_to_all(blocks, "krow", split_axis=4, concat_axis=2, tiled=True),
        "kcol",
        split_axis=5,
        concat_axis=3,
        tiled=True,
    )
    middle = whole_local(gathered, weights)
    partway = lax.all_to_all(middle, "krow", split_axis=2, concat_axis=4, tiled=True)
    returned = lax.all_to_all(partway, "kcol", split_axis=3, concat_axis=5, tiled=True)
    sigma = returned.reshape(green.shape)
    green_real = green[:, 0]
    green_imag = green[:, 1]
    self_energy_real = sigma[:, 0]
    self_energy_imaginary = sigma[:, 1]
    kern_real = (
        matmul_batch(green_real, self_energy_real) - matmul_batch(green_imag, self_energy_imaginary)
    ).astype(jnp.bfloat16)
    kern_imag = (
        matmul_batch(green_real, self_energy_imaginary) + matmul_batch(green_imag, self_energy_real)
    ).astype(jnp.bfloat16)
    corr_real = matmul_batch(kern_real, green_real) - matmul_batch(kern_imag, green_imag)
    corr_imag = matmul_batch(kern_real, green_imag) + matmul_batch(kern_imag, green_real)
    dressed_real = green_real.astype(jnp.float32) + corr_real / orbitals
    dressed_imag = green_imag.astype(jnp.float32) + corr_imag / orbitals
    dressed = jnp.stack((dressed_real, dressed_imag), 1).astype(jnp.bfloat16)
    return (sigma, dressed)


def choose(green, screened):
    devices = lax.axis_size("krow") * lax.axis_size("kcol")
    orbitals = green.shape[4]
    if orbitals % (devices * SUBLANES) == 0 and orbitals % LANES == 0:
        return exchange_in_kernel(green, screened)
    return per_device(green, screened)


def solution(mesh):
    placed = (P(None, None, "krow", "kcol", None, None), P(None, None, ("krow", "kcol")))
    return jax.shard_map(
        choose,
        mesh=mesh,
        in_specs=placed,
        out_specs=(
            P(None, None, "krow", "kcol", None, None),
            P(None, None, "krow", "kcol", None, None),
        ),
        check_vma=False,
    )
```

profile of v0, /device:TPU:15, one launch (start us, length us, event | category | flops | bytes accessed | tf_op | source)
XLA Modules:
  0.0 108.5 jit_solution(7692724018566962890)
XLA Ops:
  0.6 2.1 %reshape.17.weights = f32[16,4,8,256]{3,2,1,0:T(8,128)} reshape(f32[16,4,2048]{2,1,0:T(4,128)} %param.3) | data formatting | bytes 1048576 | tf_op jit(solution)/shard_map/reshape | solution.py:198
  2.7 101.2 %shard_map.41 = (bf16[4,2,2,256,256]{4,3,2,1,0:T(8,128)(2,1)}, bf16[4,2,2,256,256]{4,3,2,1,0:T(8,128)(2,1)}) custom-call(bf16[4,2,2,256,256]{4,3,2,1,0:T(8,128)(2,1)} %bitcast.7, f32[16,4,8,256]{3,2,1,0:T(8,128)} %reshape.17.weights), custom_call_target="tpu_custom_call" | custom-call | tf_op jit(solution)/shard_map/pallas_call | solution.py:201
  104.0 0.0 copy-start
  104.0 3.2 %copy.8 = bf16[4,2,1,2,256,256]{5,4,3,2,1,0:T(8,128)(2,1)} copy(bf16[4,2,1,2,256,256]{5,4,3,2,1,0:T(8,128)(2,1)} %bitcast.9) | data formatting | bytes 4194304
  107.2 0.0 copy-done
  107.2 1.3 %copy.9 = bf16[4,2,1,2,256,256]{5,4,3,2,1,0:T(8,128)(2,1)} copy(bf16[4,2,1,2,256,256]{5,4,3,2,1,0:T(8,128)(2,1)S(1)} %bitcast.8) | data formatting | bytes 4194304
Async XLA Ops:
  104.0 3.3 %copy-start = (bf16[4,2,2,256,256]{4,3,2,1,0:T(8,128)(2,1)S(1)}, bf16[4,2,2,256,256]{4,3,2,1,0:T(8,128)(2,1)}, u32[]{:S(2)}) copy-start(bf16[4,2,2,256,256]{4,3,2,1,0:T(8,128)(2,1)} %get-tuple-element.5) | copy-start | bytes 6291460
where the time goes:
time: 109 us
  Pallas kernels  101 us (93%)
  local copies, waits for them, and re-layouts  6.67 us (6%)
    pallas_call x1, Pallas kernels, exchange_in_kernel(): pl.pallas_call(functools.partial(kernel, grid_dims, mesh_dims, rows), out...  101 us
    unnamed x4, local copies, waits for them, and re-layouts  4.57 us

commit v1 on v0

--- a/solution.py
+++ b/solution.py
@@ -61,7 +61,7 @@
 def kernel(
     grid_dims, mesh_dims, rows,
     green, weights, sigma, dressed,
-    arrived, results, middle,
+    arrived, results, middle, pair_weights,
     out_sems, in_sems, back_out_sems, back_in_sems,
 ):
     one, two = grid_dims
@@ -114,6 +114,13 @@
         )
 
     scale = -1.0 / (one * two)
+
+    @pl.loop(0, one)
+    def _(r1):
+        for r2 in range(two):
+            for row in range(rows):
+                part = weights[r1, r2:r2 + 1, row * orbitals:(row + 1) * orbitals]
+                pair_weights[r1, r2, row:row + 1, :] = part * scale
 
     @pl.loop(0, energies)
     def _(e):
@@ -136,7 +143,7 @@
             for r1 in range(one):
                 values = transform([(middle[r1, k2, 0], middle[r1, k2, 1]) for k2 in range(two)], 1)
                 for r2 in range(two):
-                    weight = weights[r1, r2, :, lanes] * scale
+                    weight = pair_weights[r1, r2, :, lanes]
                     values[r2] = (values[r2][0] * weight, values[r2][1] * weight)
                 for k2, v in enumerate(transform(values, -1)):
                     middle[r1, k2, 0] = v[0]
@@ -195,25 +202,27 @@
     rows = orbitals // devices
     local = local_one * local_two
     flat = (energies, 2, local, orbitals, orbitals)
-    weights = screened.reshape(grid_dims + (rows, orbitals))
     block = (energies, devices, 2, local, rows, orbitals)
     vmem = pl.BlockSpec(memory_space=pltpu.VMEM)
     sigma, dressed = pl.pallas_call(
         functools.partial(kernel, grid_dims, mesh_dims, rows),
-        out_shape=[jax.ShapeDtypeStruct(flat, jnp.bfloat16)] * 2,
+        out_shape=[pltpu.VMEM(flat, jnp.bfloat16)] * 2,
         in_specs=[vmem, vmem],
         out_specs=[vmem, vmem],
         scratch_shapes=[
             pltpu.VMEM(block, jnp.bfloat16),
             pltpu.VMEM(block, jnp.bfloat16),
             pltpu.VMEM(grid_dims + (2, rows, LANES), jnp.float32),
+            pltpu.VMEM(grid_dims + (rows, orbitals), jnp.float32),
             pltpu.SemaphoreType.DMA((energies,)),
             pltpu.SemaphoreType.DMA((energies,)),
             pltpu.SemaphoreType.DMA((energies,)),
             pltpu.SemaphoreType.DMA((energies,)),
         ],
-        compiler_params=pltpu.CompilerParams(collective_id=0, has_side_effects=True),
-    )(green.reshape(flat), weights)
+        compiler_params=pltpu.CompilerParams(
+            collective_id=0, has_side_effects=True, vmem_limit_bytes=12 * math.prod(block)
+        ),
+    )(green.reshape(flat), screened)
     return sigma.reshape(green.shape), dressed.reshape(green.shape)
 
 

time: 109 us -> 104 us (0.954)
  Pallas kernels: 101 us -> 97.7 us
  local copies, waits for them, and re-layouts: 6.67 us -> 5.27 us
    pallas_call x1, Pallas kernels: 101 us -> 97.7 us  [exchange_in_kernel(): pl.pallas_call(functools.partial(kernel, grid_dims, mesh_dims, rows), out...]
    reshape x1 -> x0, local copies, waits for them, and re-layouts: 2.1 us -> none  [exchange_in_kernel(): weights = screened.reshape(grid_dims + (rows, orbitals))]
    unnamed x4 -> x6, local copies, waits for them, and re-layouts: 4.57 us -> 5.27 us
where the time goes in v1:
time: 104 us
  Pallas kernels  97.7 us (94%)
  local copies, waits for them, and re-layouts  5.27 us (5%)
    pallas_call x1, Pallas kernels, exchange_in_kernel(): pl.pallas_call(functools.partial(kernel, grid_dims, mesh_dims, rows), out...  97.7 us
    unnamed x6, local copies, waits for them, and re-layouts  5.27 us

profile of v1, /device:TPU:15, one launch (start us, length us, event | category | flops | bytes accessed | tf_op | source)
XLA Modules:
  0.0 103.6 jit_solution(14760335748094593100)
XLA Ops:
  0.6 0.0 copy-start
  0.6 1.6 %copy-done = bf16[4,2,1,2,256,256]{5,4,3,2,1,0:T(8,128)(2,1)S(1)} copy-done((bf16[4,2,1,2,256,256]{5,4,3,2,1,0:T(8,128)(2,1)S(1)}, bf16[4,2,1,2,256,256]{5,4,3,2,1,0:T(8,128)(2,1)}, u32[]{:S(2)}) %copy-start) | copy-done | bytes 2097176
  2.2 0.0 copy-start.1
  2.2 1.0 %copy-done.1 = f32[16,4,2048]{2,1,0:T(4,128)S(1)} copy-done((f32[16,4,2048]{2,1,0:T(4,128)S(1)}, f32[16,4,2048]{2,1,0:T(4,128)}, u32[]{:S(2)}) %copy-start.1) | copy-done | bytes 524312
  3.3 97.7 %shard_map.41 = (bf16[4,2,2,256,256]{4,3,2,1,0:T(8,128)(2,1)S(1)}, bf16[4,2,2,256,256]{4,3,2,1,0:T(8,128)(2,1)S(1)}) custom-call(bf16[4,2,2,256,256]{4,3,2,1,0:T(8,128)(2,1)S(1)} %bitcast.9, f32[16,4,2048]{2,1,0:T(4,128)S(1)} %copy-done.1), custom_call_target="tpu_custom_call" | custom-call | tf_op jit(solution)/shard_map/pallas_call | solution.py:207
  100.9 1.3 %copy.8 = bf16[4,2,1,2,256,256]{5,4,3,2,1,0:T(8,128)(2,1)} copy(bf16[4,2,1,2,256,256]{5,4,3,2,1,0:T(8,128)(2,1)S(1)} %bitcast.8) | data formatting | bytes 4194304
  102.2 1.3 %copy.9 = bf16[4,2,1,2,256,256]{5,4,3,2,1,0:T(8,128)(2,1)} copy(bf16[4,2,1,2,256,256]{5,4,3,2,1,0:T(8,128)(2,1)S(1)} %bitcast.7) | data formatting | bytes 4194304
Async XLA Ops:
  0.6 1.6 %copy-start = (bf16[4,2,1,2,256,256]{5,4,3,2,1,0:T(8,128)(2,1)S(1)}, bf16[4,2,1,2,256,256]{5,4,3,2,1,0:T(8,128)(2,1)}, u32[]{:S(2)}) copy-start(bf16[4,2,1,2,256,256]{5,4,3,2,1,0:T(8,128)(2,1)} %param.2) | copy-start | bytes 6291460
  2.2 1.0 %copy-start.1 = (f32[16,4,2048]{2,1,0:T(4,128)S(1)}, f32[16,4,2048]{2,1,0:T(4,128)}, u32[]{:S(2)}) copy-start(f32[16,4,2048]{2,1,0:T(4,128)} %weights.1) | copy-start | bytes 1572868
